TPU v7x, 32 devices: a whole 2x2x4 slice. The times are simulated.
32 devices in a mesh: grp: 8 (over z, x), node: 4 (over y, core).
Axes of the slice: x: 2, y: 2, z: 4, core: 2. Of those that a mesh axis runs over, the one named last changes fastest.
Arguments:
- initial: float32 [6, 32, 32768], P(None, None, ('grp', 'node')), may hold values from -0.5 to 16, as said below
- afferent_noise_level: float32 [32, 32768], P(None, ('grp', 'node')), may hold values from 0.12 to 0.32
- history: bfloat16 [64, 32, 32768], P(None, None, ('grp', 'node')), may hold values from 0 to 1
- weights: bfloat16 [32, 24, 128, 1024], P(('grp', 'node')), may hold values from -0.109375 to 0.109375
- lead_field: bfloat16 [128, 32768], P(None, ('grp', 'node')), may hold values from -0.00390625 to 0.00390625
- src_group: int32 [32, 24], replicated, may hold values from 0 to 7, as said below
- src_sub: int32 [32, 24], replicated, may hold values from 0 to 7
- delays: int32 [32, 24], replicated, may hold values from 6 to 63
- counts: int32 [32], replicated, may hold values from 16 to 24, as said below
Outputs:
- final_state: float32 [6, 32, 32768], P(None, None, ('grp', 'node'))
- sensors: float32 [6, 128, 32], replicated
Inputs may be any that keep to these rules, and one draw needn't show every extreme that they name: `initial`: rows 0 to 2 are potentials and rows 3 to 5 their rates; row 0 lies within 0 and 0.4, row 1 within 4 and 16, row 2 within 0 and 8, rows 3 to 5 within -0.5 and 0.5. `src_group`: among the tiles k < counts[b] of a block b no owner group appears more than 3 times, and some block reaches 3. Tiles k >= counts[b] of block b are ignored; in every draw some block has 24 live tiles.
All inputs are finite; a program needn't handle non-finite values.
Results may differ from a plain program's by a relative error of at most 0.0003.
The roundings to bfloat16 on the way count: a program that leaves them out, or rounds other values in their place, can miss the bound.
Values may be sent and summed in bfloat16 or wider, within the bound.
A program may use at most 128 MiB of HBM per device.

v0:
```python
import jax
import jax.numpy as jnp
from jax import lax
from jax.sharding import PartitionSpec as P

DMIN = 6
STEPS = 6
exciting_amplitude = 3.25
suppressive_amplitude = 22.0
exciting_inverse_lag = 0.1
suppressive_inverse_lag = 0.05
link_factor = 135.0
maximal_spike_frequency = 0.005
thresh = 6.0
fire_slope = 0.56
global_scaling_factor = 0.5
dt_step = 0.5


def sigmoid_spike_density(somatic_charge_level):
    return 1.0 / (1.0 + jnp.exp(fire_slope * (thresh - somatic_charge_level)))


def derivative(population_variables, afferent_noise_level, network_afferent):
    principal_cell_level, interneuron_depolarization, suppressive_depolarization = (
        population_variables[0],
        population_variables[1],
        population_variables[2],
    )
    principal_cell_curvature = (
        exciting_amplitude
        * exciting_inverse_lag
        * maximal_spike_frequency
        * sigmoid_spike_density(interneuron_depolarization - suppressive_depolarization)
        - 2.0 * exciting_inverse_lag * population_variables[3]
        - exciting_inverse_lag * exciting_inverse_lag * principal_cell_level
    )
    interneuron_second_derivative = (
        exciting_amplitude
        * exciting_inverse_lag
        * (
            afferent_noise_level
            + 0.8
            * link_factor
            * maximal_spike_frequency
            * sigmoid_spike_density(link_factor * principal_cell_level)
            + global_scaling_factor * network_afferent
        )
        - 2.0 * exciting_inverse_lag * population_variables[4]
        - exciting_inverse_lag * exciting_inverse_lag * interneuron_depolarization
    )
    suppressive_second_derivative = (
        suppressive_amplitude
        * suppressive_inverse_lag
        * 0.25
        * link_factor
        * maximal_spike_frequency
        * sigmoid_spike_density(0.25 * link_factor * principal_cell_level)
        - 2.0 * suppressive_inverse_lag * population_variables[5]
        - suppressive_inverse_lag * suppressive_inverse_lag * suppressive_depolarization
    )
    return jnp.stack(
        [
            population_variables[3],
            population_variables[4],
            population_variables[5],
            principal_cell_curvature,
            interneuron_second_derivative,
            suppressive_second_derivative,
        ]
    )


def advance(population_variables, afferent_noise_level, coupled_now, coupled_next):
    first_rate = derivative(population_variables, afferent_noise_level, coupled_now)
    second_rate = derivative(
        population_variables + dt_step * first_rate, afferent_noise_level, coupled_next
    )
    return population_variables + 0.5 * dt_step * (first_rate + second_rate)


def body(
    initial, afferent_noise_level, history, weights, lead_field, src_group, src_sub, delays, counts
):
    owners = lax.axis_size("grp")
    columns = lax.axis_size("node")
    my_group = lax.axis_index("grp")
    my_column = lax.axis_index("node")
    myself = my_group * columns + my_column
    cycle_len, replicas, block_len = history.shape
    tiles_max = src_group.shape[1]
    piece_len = weights.shape[2]
    slots_per = (tiles_max + owners - 1) // owners
    zero_index = jnp.zeros((), jnp.int32)
    tile_lanes = jnp.arange(tiles_max, dtype=jnp.int32)
    places = jnp.arange(slots_per, dtype=jnp.int32)
    tile_stack = weights.reshape(tiles_max * piece_len, block_len)

    def column_of(lookup):
        return lax.dynamic_index_in_dim(lookup.reshape(owners, columns, -1), my_column, 1, False)

    col_group = column_of(src_group)
    col_sub = column_of(src_sub)
    col_delay = column_of(delays)
    col_count = column_of(counts)[:, 0]
    matched = (col_group == my_group) & (tile_lanes[None, :] < col_count[:, None])
    ranked = jnp.cumsum(matched.astype(jnp.int32), axis=1) - 1
    picked_slot = matched[:, :, None] & (ranked[:, :, None] == places[None, None, :])
    sel_sub = jnp.sum(jnp.where(picked_slot, col_sub[:, :, None], 0), axis=1)
    sel_delay = jnp.sum(jnp.where(picked_slot, col_delay[:, :, None], 0), axis=1)
    own_group = lax.dynamic_index_in_dim(src_group, myself, 0, False)
    own_count = lax.dynamic_index_in_dim(counts, myself, 0, False)
    own_live = tile_lanes < own_count
    earlier = (
        (own_group[:, None] == own_group[None, :])
        & own_live[None, :]
        & (tile_lanes[None, :] < tile_lanes[:, None])
    )
    own_rank = jnp.minimum(jnp.sum(earlier.astype(jnp.int32), axis=1), slots_per - 1)
    own_mask = own_live.astype(jnp.bfloat16)

    def pack(cycle, in_times):
        how_many = in_times.shape[0]
        slot_ids = jnp.mod(in_times[None, :, None] - sel_delay[:, None, :], cycle_len)
        starts = jnp.broadcast_to(sel_sub[:, None, :] * piece_len, slot_ids.shape)

        def cut_piece(slot_id, start_id):
            return lax.dynamic_slice(
                cycle, (slot_id, zero_index, start_id), (1, replicas, piece_len)
            )[0]

        pieces = jax.vmap(cut_piece)(slot_ids.reshape(-1), starts.reshape(-1))
        return pieces.reshape(owners, how_many, slots_per, replicas, piece_len)

    def unpack(parcel):
        how_many = parcel.shape[1]
        picked = parcel[own_group, :, own_rank] * own_mask[:, None, None, None]
        flattened = jnp.transpose(picked, (1, 2, 0, 3)).reshape(
            how_many * replicas, tiles_max * piece_len
        )
        return jnp.dot(flattened, tile_stack, preferred_element_type=jnp.float32).reshape(
            how_many, replicas, block_len
        )

    def store_fire(cycle, population_variables, step_id):
        spike_density_result = sigmoid_spike_density(
            population_variables[1] - population_variables[2]
        ).astype(jnp.bfloat16)
        return lax.dynamic_update_slice(
            cycle, spike_density_result[None], (jnp.mod(step_id, cycle_len), zero_index, zero_index)
        )

    def record(sensors, population_variables, step_id):
        potential = (population_variables[1] - population_variables[2]).astype(jnp.bfloat16)
        local_sum = lax.dot_general(
            lead_field, potential, (((1,), (1,)), ((), ())), preferred_element_type=jnp.float32
        )
        local_sum = lax.psum(local_sum, ("grp", "node"))
        return lax.dynamic_update_slice(sensors, local_sum[None], (step_id, zero_index, zero_index))

    start_times = jnp.zeros((1,), jnp.int32)
    network_afferent = unpack(
        lax.all_to_all(pack(history, start_times), "grp", split_axis=0, concat_axis=0, tiled=True)
    )[0]
    sensors = jnp.zeros((STEPS, lead_field.shape[0], replicas), jnp.float32)

    def one_batch(batch_id, carried):
        population_variables, cycle, coupled_now, sensors = carried
        base_step = (jnp.asarray(batch_id) * DMIN).astype(jnp.int32)
        cycle = store_fire(cycle, population_variables, base_step)
        in_times = base_step + 1 + jnp.arange(DMIN, dtype=jnp.int32)
        batch_input = unpack(
            lax.all_to_all(pack(cycle, in_times), "grp", split_axis=0, concat_axis=0, tiled=True)
        )
        for offset in range(DMIN):
            step_id = base_step + offset
            if offset > 0:
                cycle = store_fire(cycle, population_variables, step_id)
            population_variables = advance(
                population_variables, afferent_noise_level, coupled_now, batch_input[offset]
            )
            coupled_now = batch_input[offset]
            sensors = record(sensors, population_variables, step_id)
        return (population_variables, cycle, coupled_now, sensors)

    population_variables, cycle, network_afferent, sensors = lax.fori_loop(
        0, STEPS // DMIN, one_batch, (initial, history, network_afferent, sensors)
    )
    return (population_variables, sensors)


def solution(mesh):
    return jax.shard_map(
        body,
        mesh=mesh,
        in_specs=(
            P(None, None, ("grp", "node")),
            P(None, ("grp", "node")),
            P(None, None, ("grp", "node")),
            P(("grp", "node"), None, None, None),
            P(None, ("grp", "node")),
            P(),
            P(),
            P(),
            P(),
        ),
        out_specs=(P(None, None, ("grp", "node")), P()),
        check_vma=False,
    )
```

profile of v0, /device:TPU:8, one launch (start us, length us, event | category | flops | bytes accessed | tf_op | source)
XLA Modules:
  0.0 292.4 jit_solution(6723610397220661307)
XLA Ops:
  7.2 0.8 reshape.515
  8.0 0.8 copy.46
  8.7 0.8 copy.44
  9.5 0.8 copy.43
  10.3 0.2 dynamic-slice_reduce_fusion.1
  10.8 0.2 select_reduce_fusion.1
  11.3 23.1 %copy.48 = bf16[64,32,1024]{1,0,2:T(8,128)(2,1)} copy(bf16[64,32,1024]{2,1,0:T(8,128)(2,1)} %param.11) | data formatting | bytes 8388608 | tf_op args[2]
  34.4 5.5 %gather_fusion = bf16[24,32,128]{1,0,2:T(8,128)(2,1)S(1)} fusion(bf16[64,32,1024]{1,0,2:T(8,128)(2,1)} %copy.48, s32[24]{0:T(128)S(1)} %fusion.184), kind=kCustom, calls=%fused_computation | custom fusion | bytes 393504 | tf_op jit(solution)/shard_map/vmap()/gather | solution.py:128
  39.9 1.1 copy.49
  41.1 6.1 %all-to-all-start = ((bf16[8,1,3,32,128]{4,3,2,1,0:T(8,128)(2,1)}), bf16[8,1,3,32,128]{4,3,2,1,0:T(8,128)(2,1)S(1)}, u32[]{:S(2)}, u32[]{:S(2)}) async-start(bf16[8,1,3,32,128]{4,3,2,1,0:T(8,128)(2,1)} %bitcast.8), calls=%async_computation | async-start | bytes 393216 | tf_op jit(solution)/shard_map/all_to_all | solution.py:163
  47.7 0.4 copy.52
  48.1 14.6 %dynamic_update_slice.38 = bf16[64,32,1024]{1,0,2:T(8,128)(2,1)} dynamic-update-slice(bf16[64,32,1024]{1,0,2:T(8,128)(2,1)} %copy.48, bf16[1,32,1024]{1,0,2:T(2,128)(2,1)S(1)} %copy.52, s32[]{:T(128)} %constant.159.clone.1, s32[]{:T(128)} %constant.159.clone.1, s32[]{:T(128)} %constant.159.clone.1) | dynamic-update-slice | bytes 131076 | tf_op jit(solution)/shard_map/while/body/eval_jaxpr/dynamic_update_slice | solution.py:149
  62.7 33.1 %gather_fusion.2 = bf16[144,32,128]{1,0,2:T(8,128)(2,1)} fusion(bf16[64,32,1024]{1,0,2:T(8,128)(2,1)} %dynamic_update_slice.38, s32[144]{0:T(256)S(1)} %bitcast.352), kind=kCustom, calls=%fused_computation.2 | custom fusion | bytes 2361024 | tf_op jit(solution)/shard_map/while/body/eval_jaxpr/vmap()/gather | solution.py:128
  95.8 7.6 %copy.55 = bf16[144,32,128]{2,1,0:T(8,128)(2,1)} copy(bf16[144,32,128]{1,0,2:T(8,128)(2,1)} %gather_fusion.2) | data formatting | bytes 2359296 | tf_op jit(solution)/shard_map/while/body/eval_jaxpr/vmap()/gather | solution.py:128
  103.3 6.1 %all-to-all-start.1 = ((bf16[8,6,3,32,128]{4,3,2,1,0:T(8,128)(2,1)}), bf16[8,6,3,32,128]{4,3,2,1,0:T(8,128)(2,1)}, u32[]{:S(2)}, u32[]{:S(2)}) async-start(bf16[8,6,3,32,128]{4,3,2,1,0:T(8,128)(2,1)} %bitcast.23), calls=%async_computation.1 | async-start | bytes 2359296 | tf_op jit(solution)/shard_map/while/body/eval_jaxpr/all_to_all | solution.py:173
  109.5 0.6 dynamic_slice.27
  110.3 0.7 fusion.185
  111.0 0.7 iota_compare_fusion.3
  111.6 0.2 convert_reduce_fusion
  111.8 0.7 gather_fusion.1
  112.6 4.0 %fusion.23 = f32[1,32,1024]{2,1,0:T(8,128)S(1)} fusion(bf16[1,24,128,1024]{3,2,1,0:T(8,128)(2,1)} %param.12, bf16[24,32,128]{2,1,0:T(8,128)(2,1)S(1)} %gather_fusion.1, f32[32,1024]{1,0:T(8,128)S(1)} %copy-done.1, f32[6,32,1024]{2,1,0:T(8,128)S(1)} %copy-done.2, bf16[24]{0:T(256)(128)(2,1)S(1)} %fusion.185), kind=kOutput, calls=%fused_computation.16 | convolution fusion | flops 201883648 | bytes 7143472 | tf_op jit(solution)/shard_map/dot_general | solution.py:141
  116.8 0.5 copy-done.8
  117.3 0.8 slice.528
  118.0 0.8 fusion.129
  118.9 16.0 %all-to-all-done.1 = bf16[8,6,3,32,128]{4,3,2,1,0:T(8,128)(2,1)} async-done(((bf16[8,6,3,32,128]{4,3,2,1,0:T(8,128)(2,1)}), bf16[8,6,3,32,128]{4,3,2,1,0:T(8,128)(2,1)}, u32[]{:S(2)}, u32[]{:S(2)}) %all-to-all-start.1) | async-done | bytes 1179680 | tf_op jit(solution)/shard_map/while/body/eval_jaxpr/all_to_all | solution.py:173
  134.8 2.1 gather_fusion.3
  137.1 0.8 copy.56
  137.9 4.2 %fusion.2 = f32[192,1024]{1,0:T(8,128)S(1)} fusion(bf16[3072,1024]{1,0:T(8,128)(2,1)} %bitcast.351, bf16[24,8,24,128]{3,2,1,0:T(8,128)(2,1)S(1)} %bitcast.353), kind=kOutput, calls=%fused_computation.6 | convolution fusion | flops 1207959552 | bytes 8257536 | tf_op jit(solution)/shard_map/while/body/eval_jaxpr/dot_general | solution.py:141
  142.3 0.2 fusion.27
  143.2 0.8 convolution_bitcast_fusion.5
  144.0 0.2 fusion.29
  144.2 0.8 convolution_bitcast_fusion.4
  145.6 0.2 fusion.31
  145.9 0.8 convolution_bitcast_fusion.3
  147.3 0.2 fusion.33
  147.5 0.8 convolution_bitcast_fusion.2
  148.9 0.2 fusion.35
  149.2 0.8 convolution_bitcast_fusion.1
  150.6 0.2 fusion.37
  150.8 0.8 convolution_bitcast_fusion
  151.7 128.9 %all-reduce.4.cloned.1.call-done = (f32[1,128,32]{1,2,0:T(8,128)}, f32[1,128,32]{1,2,0:T(8,128)}, f32[1,128,32]{1,2,0:T(8,128)}, f32[1,128,32]{1,2,0:T(8,128)}, ...) async-done(((f32[1,128,32]{1,2,0:T(8,128)}, f32[1,128,32]{1,2,0:T(8,128)}, f32[1,128,32]{1,2,0:T(8,128)}, f32[1,128,32]{1,2,0:T(8,128)}, f32[1,128,32]{1,2,0:T(8,128)}, ...) | async-done | bytes 98320 | tf_op jit(solution)/shard_map/while/body/eval_jaxpr/psum | solution.py:158
  280.6 0.7 dynamic_update_slice.39
  281.4 0.7 constant_dynamic-update-slice_fusion.3
  282.1 0.7 constant_dynamic-update-slice_fusion.2
  282.8 0.7 constant_dynamic-update-slice_fusion.1
  283.5 0.7 constant_dynamic-update-slice_fusion
  284.2 0.7 constant_dynamic-update-slice_fusion.4
  285.0 0.6 copy-done.13
  (94 shorter events, 4.7 us)
Async XLA Ops:
  7.2 136.0 %copy-start = (bf16[128,1024]{1,0:T(8,128)(2,1)S(1)}, bf16[128,1024]{1,0:T(8,128)(2,1)}, u32[]{:S(2)}) copy-start(bf16[128,1024]{1,0:T(8,128)(2,1)} %param.13) | copy-start | bytes 786436
  39.9 7.6 %copy-start.2 = (f32[6,32,1024]{2,1,0:T(8,128)S(1)}, f32[6,32,1024]{2,1,0:T(8,128)}, u32[]{:S(2)}) copy-start(f32[6,32,1024]{2,1,0:T(8,128)} %param.9) | copy-start | bytes 2359300
  41.1 62.3 %all-to-all-start = ((bf16[8,1,3,32,128]{4,3,2,1,0:T(8,128)(2,1)}), bf16[8,1,3,32,128]{4,3,2,1,0:T(8,128)(2,1)S(1)}, u32[]{:S(2)}, u32[]{:S(2)}) async-start(bf16[8,1,3,32,128]{4,3,2,1,0:T(8,128)(2,1)} %bitcast.8), calls=%async_computation | async-start | bytes 393216 | tf_op jit(solution)/shard_map/all_to_all | solution.py:163
  47.7 68.9 %copy-start.4 = (f32[1,32,1024]{2,1,0:T(8,128)}, f32[1,32,1024]{2,1,0:T(8,128)S(1)}, u32[]{:S(2)}) copy-start(f32[1,32,1024]{2,1,0:T(8,128)S(1)} %get-tuple-element.77) | copy-start | bytes 393220
  47.7 68.9 %copy-start.6 = (f32[1,32,1024]{2,1,0:T(8,128)}, f32[1,32,1024]{2,1,0:T(8,128)S(1)}, u32[]{:S(2)}) copy-start(f32[1,32,1024]{2,1,0:T(8,128)S(1)} %get-tuple-element.78) | copy-start | bytes 393220
  103.3 6.2 %copy-start.15 = (s32[32]{0:T(128)S(1)}, s32[32]{0:T(128)}, u32[]{:S(2)}) copy-start(s32[32]{0:T(128)} %param.17) | copy-start | bytes 388
  103.3 6.8 %copy-start.14 = (s32[32,24]{0,1:T(8,128)S(1)}, s32[32,24]{0,1:T(8,128)}, u32[]{:S(2)}) copy-start(s32[32,24]{0,1:T(8,128)} %param.14) | copy-start | bytes 9220
  103.3 31.5 %all-to-all-start.1 = ((bf16[8,6,3,32,128]{4,3,2,1,0:T(8,128)(2,1)}), bf16[8,6,3,32,128]{4,3,2,1,0:T(8,128)(2,1)}, u32[]{:S(2)}, u32[]{:S(2)}) async-start(bf16[8,6,3,32,128]{4,3,2,1,0:T(8,128)(2,1)} %bitcast.23), calls=%async_computation.1 | async-start | bytes 2359296 | tf_op jit(solution)/shard_map/while/body/eval_jaxpr/all_to_all | solution.py:173
  109.5 3.1 %copy-start.1 = (f32[32,1024]{1,0:T(8,128)S(1)}, f32[32,1024]{1,0:T(8,128)}, u32[]{:S(2)}) copy-start(f32[32,1024]{1,0:T(8,128)} %param.10) | copy-start | bytes 393220
  109.5 171.1 %all-reduce.4.cloned.1.call-start = ((), (), s32[]{:S(2)}) async-start(), calls=%async_computation.2 | async-start | bytes 196608 | tf_op jit(solution)/shard_map/while/body/eval_jaxpr/psum | solution.py:158
  116.6 0.7 copy-start.8
  137.9 4.4 %copy-start.3 = (f32[3,32,1024]{2,1,0:T(8,128)S(1)}, f32[3,32,1024]{2,1,0:T(8,128)}, u32[]{:S(2)}) copy-start(f32[3,32,1024]{2,1,0:T(8,128)} %slice.528) | copy-start | bytes 1179652
  137.9 4.4 %copy-start.5 = (f32[1,32,1024]{2,1,0:T(8,128)S(1)}, f32[1,32,1024]{2,1,0:T(8,128)}, u32[]{:S(2)}) copy-start(f32[1,32,1024]{2,1,0:T(8,128)} %copy-done.4) | copy-start | bytes 393220
  137.9 4.4 %copy-start.7 = (f32[1,32,1024]{2,1,0:T(8,128)S(1)}, f32[1,32,1024]{2,1,0:T(8,128)}, u32[]{:S(2)}) copy-start(f32[1,32,1024]{2,1,0:T(8,128)} %copy-done.6) | copy-start | bytes 393220
  137.9 4.4 %copy-start.9 = (f32[1,32,1024]{2,1,0:T(8,128)S(1)}, f32[1,32,1024]{2,1,0:T(8,128)}, u32[]{:S(2)}) copy-start(f32[1,32,1024]{2,1,0:T(8,128)} %copy-done.8) | copy-start | bytes 393220
  137.9 4.4 %copy-start.11 = (f32[1,32,1024]{2,1,0:T(8,128)S(1)}, f32[1,32,1024]{2,1,0:T(8,128)}, u32[]{:S(2)}) copy-start(f32[1,32,1024]{2,1,0:T(8,128)} %get-tuple-element.74) | copy-start | bytes 393220
  137.9 4.4 %copy-start.12 = (f32[1,32,1024]{2,1,0:T(8,128)S(1)}, f32[1,32,1024]{2,1,0:T(8,128)}, u32[]{:S(2)}) copy-start(f32[1,32,1024]{2,1,0:T(8,128)} %get-tuple-element.75) | copy-start | bytes 393220
  150.8 134.1 %copy-start.10 = (f32[6,32,1024]{2,1,0:T(8,128)}, f32[6,32,1024]{2,1,0:T(8,128)S(1)}, u32[]{:S(2)}) copy-start(f32[6,32,1024]{2,1,0:T(8,128)S(1)} %fusion.37) | copy-start | bytes 2359300
  285.0 0.6 copy-start.13
Sparse Core Ops, SparseCore 0:
  151.8 128.7 all-reduce.3
where the time goes:
time: 294 us; the launch traced here: 292 us
  waiting for transfers between devices  145 us (49%)
  local copies, waits for them, and re-layouts  100 us (34%)
  between operations  14.7 us (5%)
  matrix products  13.1 us (4%)
  starting transfers between devices  12.2 us (4%)
  other arithmetic  7.27 us (2%)
    psum x1, waiting for transfers between devices, record(): local_sum = lax.psum(local_sum, ('grp', 'node'))  129 us
    gather x4, local copies, waits for them, and re-layouts, cut_piece(): lax.dynamic_slice(cycle, (slot_id, zero_index, start_id), (1, replicas, p...  47.3 us
    unnamed x36, local copies, waits for them, and re-layouts  26.6 us
    all_to_all x1, waiting for transfers between devices, one_batch(): lax.all_to_all(pack(cycle, in_times), 'grp', split_axis=0, concat_axis=0,...  16 us
    dynamic_update_slice x1, local copies, waits for them, and re-layouts, store_fire(): lax.dynamic_update_slice(cycle, spike_density_result[None], (jnp.mod(step...  14.6 us
    dot_general x2, matrix products, unpack(): jnp.dot(flattened, tile_stack, preferred_element_type=jnp.float32)  8.29 us
    all_to_all x1, starting transfers between devices, one_batch(): lax.all_to_all(pack(cycle, in_times), 'grp', split_axis=0, concat_axis=0,...  6.14 us
    all_to_all x1, starting transfers between devices, body(): lax.all_to_all(pack(history, start_times), 'grp', split_axis=0, concat_ax...  6.07 us
  transfers between devices with their start and end apart: 3, of which 2 were waited for; matrix products, arithmetic and copies ran while one was open for 22% of the time, Pallas kernels for 0%

commit v1 on v0

--- a/solution.py
+++ b/solution.py
@@ -155,7 +155,7 @@
         local_sum = lax.dot_general(
             lead_field, potential, (((1,), (1,)), ((), ())), preferred_element_type=jnp.float32
         )
-        local_sum = lax.psum(local_sum, ("grp", "node"))
+        local_sum = jnp.sum(lax.all_gather(local_sum, ("grp", "node")), axis=0)
         return lax.dynamic_update_slice(sensors, local_sum[None], (step_id, zero_index, zero_index))
 
     start_times = jnp.zeros((1,), jnp.int32)

time: 294 us -> 384 us (1.31)
  the two profiles are of different devices: /device:TPU:8 before, /device:TPU:0 now
where the time goes in v1:
time: 384 us; the launch traced here: 383 us
  blocking collectives  235 us (61%)
  local copies, waits for them, and re-layouts  97.8 us (25%)
  waiting for transfers between devices  18.9 us (5%)
  starting transfers between devices  13 us (3%)
  matrix products  9.38 us (2%)
  other arithmetic  7.69 us (2%)
    all_gather x6, blocking collectives, record(): local_sum = jnp.sum(lax.all_gather(local_sum, ('grp', 'node')), axis=0)  235 us
    gather x4, local copies, waits for them, and re-layouts, cut_piece(): lax.dynamic_slice(cycle, (slot_id, zero_index, start_id), (1, replicas, p...  47.9 us
    unnamed x44, local copies, waits for them, and re-layouts  27.9 us
    all_to_all x1, waiting for transfers between devices, one_batch(): lax.all_to_all(pack(cycle, in_times), 'grp', split_axis=0, concat_axis=0,...  18.9 us
    dynamic_update_slice x1, local copies, waits for them, and re-layouts, store_fire(): lax.dynamic_update_slice(cycle, spike_density_result[None], (jnp.mod(step...  14.6 us
    dot_general x2, matrix products, unpack(): jnp.dot(flattened, tile_stack, preferred_element_type=jnp.float32)  8.29 us
  transfers between devices with their start and end apart: 2, of which 1 were waited for; matrix products, arithmetic and copies ran while one was open for 17% of the time, Pallas kernels for 0%

profile of v1, /device:TPU:0, one launch (start us, length us, event | category | flops | bytes accessed | tf_op | source)
XLA Modules:
  0.0 382.9 jit_solution(7776598898308544330)
XLA Ops:
  0.7 0.8 reshape.515
  1.4 0.8 copy.46
  2.2 0.8 copy.44
  3.0 0.8 copy.43
  3.8 0.2 dynamic-slice_reduce_fusion.1
  4.2 0.2 select_reduce_fusion.1
  4.8 23.1 %copy.48 = bf16[64,32,1024]{1,0,2:T(8,128)(2,1)} copy(bf16[64,32,1024]{2,1,0:T(8,128)(2,1)} %param.11) | data formatting | bytes 8388608 | tf_op args[2]
  27.9 5.8 %gather_fusion = bf16[24,32,128]{1,0,2:T(8,128)(2,1)S(1)} fusion(bf16[64,32,1024]{1,0,2:T(8,128)(2,1)} %copy.48, s32[24]{0:T(128)S(1)} %fusion.184), kind=kCustom, calls=%fused_computation | custom fusion | bytes 393504 | tf_op jit(solution)/shard_map/vmap()/gather | solution.py:128
  33.7 1.1 copy.49
  34.8 7.2 %all-to-all-start = ((bf16[8,1,3,32,128]{4,3,2,1,0:T(8,128)(2,1)}), bf16[8,1,3,32,128]{4,3,2,1,0:T(8,128)(2,1)S(1)}, u32[]{:S(2)}, u32[]{:S(2)}) async-start(bf16[8,1,3,32,128]{4,3,2,1,0:T(8,128)(2,1)} %bitcast.8), calls=%async_computation | async-start | bytes 393216 | tf_op jit(solution)/shard_map/all_to_all | solution.py:163
  42.6 0.4 copy.52
  43.0 14.6 %dynamic_update_slice.38 = bf16[64,32,1024]{1,0,2:T(8,128)(2,1)} dynamic-update-slice(bf16[64,32,1024]{1,0,2:T(8,128)(2,1)} %copy.48, bf16[1,32,1024]{1,0,2:T(2,128)(2,1)S(1)} %copy.52, s32[]{:T(128)} %constant.161.clone.1, s32[]{:T(128)} %constant.161.clone.1, s32[]{:T(128)} %constant.161.clone.1) | dynamic-update-slice | bytes 131076 | tf_op jit(solution)/shard_map/while/body/eval_jaxpr/dynamic_update_slice | solution.py:149
  57.6 33.4 %gather_fusion.2 = bf16[144,32,128]{1,0,2:T(8,128)(2,1)} fusion(bf16[64,32,1024]{1,0,2:T(8,128)(2,1)} %dynamic_update_slice.38, s32[144]{0:T(256)S(1)} %bitcast.381), kind=kCustom, calls=%fused_computation.2 | custom fusion | bytes 2361024 | tf_op jit(solution)/shard_map/while/body/eval_jaxpr/vmap()/gather | solution.py:128
  91.0 7.6 %copy.55 = bf16[144,32,128]{2,1,0:T(8,128)(2,1)} copy(bf16[144,32,128]{1,0,2:T(8,128)(2,1)} %gather_fusion.2) | data formatting | bytes 2359296 | tf_op jit(solution)/shard_map/while/body/eval_jaxpr/vmap()/gather | solution.py:128
  98.6 5.8 %all-to-all-start.1 = ((bf16[8,6,3,32,128]{4,3,2,1,0:T(8,128)(2,1)}), bf16[8,6,3,32,128]{4,3,2,1,0:T(8,128)(2,1)}, u32[]{:S(2)}, u32[]{:S(2)}) async-start(bf16[8,6,3,32,128]{4,3,2,1,0:T(8,128)(2,1)} %bitcast.23), calls=%async_computation.1 | async-start | bytes 2359296 | tf_op jit(solution)/shard_map/while/body/eval_jaxpr/all_to_all | solution.py:173
  104.4 0.6 dynamic_slice.27
  105.2 0.7 fusion.185
  105.9 0.7 iota_compare_fusion.3
  106.5 0.2 convert_reduce_fusion
  106.7 0.7 gather_fusion.1
  107.5 4.0 %fusion.23 = f32[1,32,1024]{2,1,0:T(8,128)S(1)} fusion(bf16[1,24,128,1024]{3,2,1,0:T(8,128)(2,1)} %param.12, bf16[24,32,128]{2,1,0:T(8,128)(2,1)S(1)} %gather_fusion.1, f32[32,1024]{1,0:T(8,128)S(1)} %copy-done.1, f32[6,32,1024]{2,1,0:T(8,128)S(1)} %copy-done.2, bf16[24]{0:T(256)(128)(2,1)S(1)} %fusion.185), kind=kOutput, calls=%fused_computation.16 | convolution fusion | flops 201883648 | bytes 7143472 | tf_op jit(solution)/shard_map/dot_general | solution.py:141
  111.7 0.5 copy-done.9
  112.2 0.8 slice.528
  112.9 0.8 fusion.129
  113.8 18.9 %all-to-all-done.1 = bf16[8,6,3,32,128]{4,3,2,1,0:T(8,128)(2,1)} async-done(((bf16[8,6,3,32,128]{4,3,2,1,0:T(8,128)(2,1)}), bf16[8,6,3,32,128]{4,3,2,1,0:T(8,128)(2,1)}, u32[]{:S(2)}, u32[]{:S(2)}) %all-to-all-start.1) | async-done | bytes 1179680 | tf_op jit(solution)/shard_map/while/body/eval_jaxpr/all_to_all | solution.py:173
  132.7 2.1 gather_fusion.3
  135.0 0.8 copy.56
  135.8 4.2 %fusion.2 = f32[192,1024]{1,0:T(8,128)S(1)} fusion(bf16[3072,1024]{1,0:T(8,128)(2,1)} %bitcast.380, bf16[24,8,24,128]{3,2,1,0:T(8,128)(2,1)S(1)} %bitcast.388), kind=kOutput, calls=%fused_computation.6 | convolution fusion | flops 1207959552 | bytes 8257536 | tf_op jit(solution)/shard_map/while/body/eval_jaxpr/dot_general | solution.py:141
  140.2 0.2 fusion.27
  141.0 0.2 convolution_bitcast_fusion.5
  141.2 0.2 fusion.29
  141.5 0.2 convolution_bitcast_fusion.4
  142.3 0.2 fusion.31
  142.5 0.2 convolution_bitcast_fusion.3
  143.3 0.2 fusion.33
  143.6 0.2 convolution_bitcast_fusion.2
  144.4 0.2 fusion.35
  144.6 0.2 convolution_bitcast_fusion.1
  145.4 0.7 copy-done.3
  146.1 41.6 %all-gather = f32[4096,32]{0,1:T(8,128)S(1)} all-gather(f32[128,32]{0,1:T(8,128)S(1)} %convolution_bitcast_fusion.5), channel_id=2, replica_groups=mesh['grp'=8,'node'=4] {'grp','node'}, dimensions={0}, use_global_device_ids=true | all-gather | bytes 540672 | tf_op jit(solution)/shard_map/while/body/eval_jaxpr/all_gather | solution.py:158
  187.9 38.1 %all-gather.1 = f32[4096,32]{0,1:T(8,128)S(1)} all-gather(f32[128,32]{0,1:T(8,128)S(1)} %convolution_bitcast_fusion.4), channel_id=3, replica_groups=mesh['grp'=8,'node'=4] {'grp','node'}, dimensions={0}, use_global_device_ids=true | all-gather | bytes 540672 | tf_op jit(solution)/shard_map/while/body/eval_jaxpr/all_gather | solution.py:158
  226.1 39.4 %all-gather.2 = f32[4096,32]{0,1:T(8,128)S(1)} all-gather(f32[128,32]{0,1:T(8,128)S(1)} %convolution_bitcast_fusion.3), channel_id=4, replica_groups=mesh['grp'=8,'node'=4] {'grp','node'}, dimensions={0}, use_global_device_ids=true | all-gather | bytes 540672 | tf_op jit(solution)/shard_map/while/body/eval_jaxpr/all_gather | solution.py:158
  265.6 38.1 %all-gather.3 = f32[4096,32]{0,1:T(8,128)S(1)} all-gather(f32[128,32]{0,1:T(8,128)S(1)} %convolution_bitcast_fusion.2), channel_id=5, replica_groups=mesh['grp'=8,'node'=4] {'grp','node'}, dimensions={0}, use_global_device_ids=true | all-gather | bytes 540672 | tf_op jit(solution)/shard_map/while/body/eval_jaxpr/all_gather | solution.py:158
  303.9 39.5 %all-gather.4 = f32[4096,32]{0,1:T(8,128)S(1)} all-gather(f32[128,32]{0,1:T(8,128)S(1)} %convolution_bitcast_fusion.1), channel_id=6, replica_groups=mesh['grp'=8,'node'=4] {'grp','node'}, dimensions={0}, use_global_device_ids=true | all-gather | bytes 540672 | tf_op jit(solution)/shard_map/while/body/eval_jaxpr/all_gather | solution.py:158
  343.6 0.2 fusion.37
  343.8 0.2 convolution_bitcast_fusion
  344.0 38.1 %all-gather.5 = f32[4096,32]{0,1:T(8,128)S(1)} all-gather(f32[128,32]{0,1:T(8,128)S(1)} %convolution_bitcast_fusion), channel_id=7, replica_groups=mesh['grp'=8,'node'=4] {'grp','node'}, dimensions={0}, use_global_device_ids=true | all-gather | bytes 540672 | tf_op jit(solution)/shard_map/while/body/eval_jaxpr/all_gather | solution.py:158
  382.3 0.6 copy-done.14
  (112 shorter events, 5.6 us)
Async XLA Ops:
  0.6 140.4 %copy-start = (bf16[128,1024]{1,0:T(8,128)(2,1)S(1)}, bf16[128,1024]{1,0:T(8,128)(2,1)}, u32[]{:S(2)}) copy-start(bf16[128,1024]{1,0:T(8,128)(2,1)} %param.13) | copy-start | bytes 786436
  33.7 8.8 %copy-start.2 = (f32[6,32,1024]{2,1,0:T(8,128)S(1)}, f32[6,32,1024]{2,1,0:T(8,128)}, u32[]{:S(2)}) copy-start(f32[6,32,1024]{2,1,0:T(8,128)} %param.9) | copy-start | bytes 2359300
  34.8 63.8 %all-to-all-start = ((bf16[8,1,3,32,128]{4,3,2,1,0:T(8,128)(2,1)}), bf16[8,1,3,32,128]{4,3,2,1,0:T(8,128)(2,1)S(1)}, u32[]{:S(2)}, u32[]{:S(2)}) async-start(bf16[8,1,3,32,128]{4,3,2,1,0:T(8,128)(2,1)} %bitcast.8), calls=%async_computation | async-start | bytes 393216 | tf_op jit(solution)/shard_map/all_to_all | solution.py:163
  42.6 68.9 %copy-start.5 = (f32[1,32,1024]{2,1,0:T(8,128)}, f32[1,32,1024]{2,1,0:T(8,128)S(1)}, u32[]{:S(2)}) copy-start(f32[1,32,1024]{2,1,0:T(8,128)S(1)} %get-tuple-element.71) | copy-start | bytes 393220
  42.6 68.9 %copy-start.7 = (f32[1,32,1024]{2,1,0:T(8,128)}, f32[1,32,1024]{2,1,0:T(8,128)S(1)}, u32[]{:S(2)}) copy-start(f32[1,32,1024]{2,1,0:T(8,128)S(1)} %get-tuple-element.72) | copy-start | bytes 393220
  98.6 5.8 %copy-start.16 = (s32[32]{0:T(128)S(1)}, s32[32]{0:T(128)}, u32[]{:S(2)}) copy-start(s32[32]{0:T(128)} %param.17) | copy-start | bytes 388
  98.6 6.4 %copy-start.15 = (s32[32,24]{0,1:T(8,128)S(1)}, s32[32,24]{0,1:T(8,128)}, u32[]{:S(2)}) copy-start(s32[32,24]{0,1:T(8,128)} %param.14) | copy-start | bytes 9220
  98.6 34.1 %all-to-all-start.1 = ((bf16[8,6,3,32,128]{4,3,2,1,0:T(8,128)(2,1)}), bf16[8,6,3,32,128]{4,3,2,1,0:T(8,128)(2,1)}, u32[]{:S(2)}, u32[]{:S(2)}) async-start(bf16[8,6,3,32,128]{4,3,2,1,0:T(8,128)(2,1)} %bitcast.23), calls=%async_computation.1 | async-start | bytes 2359296 | tf_op jit(solution)/shard_map/while/body/eval_jaxpr/all_to_all | solution.py:173
  104.4 3.1 copy-start.1
  111.5 0.7 copy-start.9
  135.7 4.4 %copy-start.4 = (f32[3,32,1024]{2,1,0:T(8,128)S(1)}, f32[3,32,1024]{2,1,0:T(8,128)}, u32[]{:S(2)}) copy-start(f32[3,32,1024]{2,1,0:T(8,128)} %slice.528) | copy-start | bytes 1179652
  135.7 4.4 %copy-start.6 = (f32[1,32,1024]{2,1,0:T(8,128)S(1)}, f32[1,32,1024]{2,1,0:T(8,128)}, u32[]{:S(2)}) copy-start(f32[1,32,1024]{2,1,0:T(8,128)} %copy-done.5) | copy-start | bytes 393220
  135.7 4.4 %copy-start.8 = (f32[1,32,1024]{2,1,0:T(8,128)S(1)}, f32[1,32,1024]{2,1,0:T(8,128)}, u32[]{:S(2)}) copy-start(f32[1,32,1024]{2,1,0:T(8,128)} %copy-done.7) | copy-start | bytes 393220
  135.8 4.4 %copy-start.10 = (f32[1,32,1024]{2,1,0:T(8,128)S(1)}, f32[1,32,1024]{2,1,0:T(8,128)}, u32[]{:S(2)}) copy-start(f32[1,32,1024]{2,1,0:T(8,128)} %copy-done.9) | copy-start | bytes 393220
  135.8 4.4 %copy-start.12 = (f32[1,32,1024]{2,1,0:T(8,128)S(1)}, f32[1,32,1024]{2,1,0:T(8,128)}, u32[]{:S(2)}) copy-start(f32[1,32,1024]{2,1,0:T(8,128)} %get-tuple-element.68) | copy-start | bytes 393220
  135.8 4.4 %copy-start.13 = (f32[1,32,1024]{2,1,0:T(8,128)S(1)}, f32[1,32,1024]{2,1,0:T(8,128)}, u32[]{:S(2)}) copy-start(f32[1,32,1024]{2,1,0:T(8,128)} %get-tuple-element.69) | copy-start | bytes 393220
  145.2 0.9 copy-start.3
  303.9 39.7 %slice-start = ((f32[6,32,1024]{2,1,0:T(8,128)}), f32[3,32,1024]{2,1,0:T(8,128)S(1)}, s32[]{:S(2)}) async-start(f32[6,32,1024]{2,1,0:T(8,128)} %copy-done.3), calls=%async_computation.2 | async-start | bytes 786432 | tf_op jit(solution)/shard_map/while/body/eval_jaxpr/slice | solution.py:64
  343.8 38.4 %copy-start.11 = (f32[6,32,1024]{2,1,0:T(8,128)}, f32[6,32,1024]{2,1,0:T(8,128)S(1)}, u32[]{:S(2)}) copy-start(f32[6,32,1024]{2,1,0:T(8,128)S(1)} %fusion.37) | copy-start | bytes 2359300
  382.3 0.6 copy-start.14
